TPU v7x, 32 devices: a whole 2x2x4 slice. The times are simulated.
32 devices in a mesh: row: 8 (over z, x), mem: 2 (over core), lev: 2 (over y).
Axes of the slice: x: 2, y: 2, z: 4, core: 2. Of those that a mesh axis runs over, the one named last changes fastest.
Arguments:
- control_fields: bfloat16 [4, 6, 256, 2048], P('mem', 'lev', 'row'), may hold values from -6 to 6
- perturbations: bfloat16 [3, 4, 6, 256, 2048], P(None, 'mem', 'lev', 'row'), may hold values from -3 to 3
- column_taper: bfloat16 [2048, 2048], P('row'), may hold values from -1 to 2, as said below
- row_taper: bfloat16 [256, 256], P('row'), may hold values from -1 to 2, as said below
- courant_numbers: float32 [3, 6, 256, 2048], P(None, 'lev', 'row', 'mem'), may hold values from -0.3 to 0.3
- tracer_slope: float32 [2, 6, 256, 2048], P(None, 'lev', 'row', 'mem'), may hold values from -3 to 3
Outputs:
- increment: float32 [3, 6, 256, 2048], P(None, 'lev', 'row', 'mem')
Inputs may be any that keep to these rules, and one draw needn't show every extreme that they name: `column_taper`: A square matrix. `row_taper`: A square matrix.
All inputs are finite; a program needn't handle non-finite values.
Results may differ from a plain program's by a relative error of at most 0.0048.
Values may be sent and summed in bfloat16 or wider, within the bound.
A program may use at most 64 MiB of HBM per device.

v0:
```python
import jax
import jax.numpy as jnp
from jax import lax
from jax.sharding import PartitionSpec as P

STEPS = 4


def faces(block, axis, dim):
    count = lax.axis_size(axis)
    forward = [(i, i + 1) for i in range(count - 1)]
    backward = [(target, source) for source, target in forward]
    last = block.shape[dim]
    low = lax.ppermute(lax.slice_in_dim(block, last - 1, last, axis=dim), axis, forward)
    high = lax.ppermute(lax.slice_in_dim(block, 0, 1, axis=dim), axis, backward)
    return (low, high)


def advance(present, courant_numbers, tracer_slope):
    change = 0.0
    ends = [faces(present, axis, dim) for axis, dim in (("lev", 1), ("row", 2), ("mem", 3))]
    for at, (low, high) in enumerate(ends):
        dim = at + 1
        size = present.shape[dim]
        behind = jnp.concatenate([low, lax.slice_in_dim(present, 0, size - 1, axis=dim)], axis=dim)
        forward = jnp.concatenate([lax.slice_in_dim(present, 1, size, axis=dim), high], axis=dim)
        velocity = courant_numbers[at]
        change = change + (
            jnp.maximum(velocity, 0.0) * (present - behind)
            + jnp.minimum(velocity, 0.0) * (forward - present)
        )
    shifted = present - change
    source = present[0] * tracer_slope[0] + present[1] * tracer_slope[1]
    return jnp.concatenate([shifted[:2], shifted[2:] - source[None]], axis=0)


def on_device(
    control_fields, perturbations, column_taper, row_taper, courant_numbers, tracer_slope
):
    member_count, level_count, row_count, column_count = control_fields.shape
    field_count = member_count * level_count
    mem_count = lax.axis_size("mem")
    mem_at = lax.axis_index("mem")
    width = column_count // mem_count
    own_block = lax.dynamic_slice_in_dim(column_taper, mem_at * width, width, 1)
    taper_columns = lax.all_gather(own_block, "row", axis=0, tiled=True)
    row_whole = lax.all_gather(row_taper, "row", axis=0, tiled=True)
    fields = control_fields.reshape(field_count, row_count, column_count)
    tapered = jnp.einsum(
        "ij,fjc->fic",
        row_whole,
        lax.all_to_all(fields, "row", split_axis=2, concat_axis=1, tiled=True),
        preferred_element_type=jnp.float32,
    )
    tapered = lax.all_to_all(
        tapered.astype(jnp.bfloat16), "row", split_axis=1, concat_axis=2, tiled=True
    )
    weighted = 0.0
    for shift in range(mem_count):
        ring = [(i, (i + shift) % mem_count) for i in range(mem_count)]
        target = lax.rem(mem_at + shift, mem_count)
        part = lax.dynamic_slice_in_dim(perturbations, target * width, width, 4)
        half = tapered
        if shift:
            part = lax.ppermute(part, "mem", ring)
            half = lax.ppermute(half, "mem", ring)
        localized = jnp.dot(
            half.reshape(field_count * row_count, column_count),
            taper_columns,
            preferred_element_type=jnp.float32,
        ).reshape(member_count, level_count, row_count, width)
        for m in range(member_count):
            weighted = weighted + part[:, m].astype(jnp.float32) * localized[m][None]
    present = weighted
    for advect_step in range(STEPS):
        present = advance(present, courant_numbers, tracer_slope)
    return present


def solution(mesh):
    placed = (
        P("mem", "lev", "row", None),
        P(None, "mem", "lev", "row", None),
        P("row", None),
        P("row", None),
        P(None, "lev", "row", "mem"),
        P(None, "lev", "row", "mem"),
    )
    return jax.shard_map(
        on_device,
        mesh=mesh,
        in_specs=placed,
        out_specs=P(None, "lev", "row", "mem"),
        check_vma=False,
    )
```

profile of v0, /device:TPU:13, one launch (start us, length us, event | category | flops | bytes accessed | tf_op | source)
XLA Modules:
  0.0 221.7 jit_solution(6026272361632896268)
XLA Ops:
  8.6 4.2 %copy.27 = bf16[6,32,2048]{1,0,2:T(8,128)(2,1)} copy(bf16[6,32,2048]{2,1,0:T(8,128)(2,1)S(1)} %bitcast.79) | data formatting | bytes 1572864 | tf_op jit(solution)/shard_map/reshape | solution.py:48
  12.9 5.7 %reshape.36 = bf16[8,2,24576]{2,1,0:T(2,128)(2,1)} reshape(bf16[2048,6,32]{2,1,0:T(8,128)(2,1)} %bitcast.70) | data formatting | bytes 1572864
  18.6 5.8 %all-to-all-start = ((bf16[8,2,24576]{2,1,0:T(2,128)(2,1)}), bf16[8,2,24576]{2,1,0:T(2,128)(2,1)S(1)}, u32[]{:S(2)}, u32[]{:S(2)}) async-start(bf16[8,2,24576]{2,1,0:T(2,128)(2,1)} %reshape.36), calls=%async_computation | async-start | bytes 1572864 | tf_op jit(solution)/shard_map/all_to_all | solution.py:52
  24.4 47.8 %all_gather.6 = bf16[256,256]{1,0:T(8,128)(2,1)S(1)} all-gather(bf16[32,256]{1,0:T(8,128)(2,1)S(1)} %copy-done.6), channel_id=1, replica_groups=mesh['row'=8,'mem'=2,'lev'=2] {'row'}, dimensions={0}, use_global_device_ids=true | all-gather | bytes 147456 | tf_op jit(solution)/shard_map/all_gather | solution.py:47
  72.2 4.2 %reshape.37 = bf16[2048,6,32]{2,1,0:T(8,128)(2,1)} reshape(bf16[8,2,24576]{2,1,0:T(2,128)(2,1)S(1)} %all-to-all-done) | data formatting | bytes 1572864
  76.4 4.1 %copy.29 = bf16[6,8,32,256]{3,2,1,0:T(8,128)(2,1)S(1)} copy(bf16[6,8,32,256]{2,0,3,1:T(8,128)(2,1)} %bitcast.69) | data formatting | bytes 1572864 | tf_op jit(solution)/shard_map/all_to_all | solution.py:52
  80.9 1.8 copy.31
  82.7 4.6 %all-to-all-start.1 = ((bf16[6,256,256]{2,0,1:T(8,128)(2,1)}), bf16[6,256,256]{2,0,1:T(8,128)(2,1)S(1)}, u32[]{:S(2)}, u32[]{:S(2)}) async-start(bf16[6,256,256]{2,0,1:T(8,128)(2,1)} %copy.31), calls=%async_computation.1 | async-start | bytes 2097152 | tf_op jit(solution)/shard_map/all_to_all | solution.py:55
  87.2 1.4 constant_dynamic-slice_fusion
  89.8 6.7 %collective-permute-start = (bf16[3,2,3,32,1024]{4,3,2,0,1:T(8,128)(2,1)}, bf16[3,2,3,32,1024]{4,3,2,0,1:T(8,128)(2,1)}, u32[]{:S(2)}, u32[]{:S(2)}) collective-permute-start(bf16[3,2,3,32,1024]{4,3,2,0,1:T(8,128)(2,1)} %copy.44), channel_id=1, source_target_pairs={{0,2},{2,0},{1,3},{3,1},{4,6},{6,4},{5,7},{7,5},{8,10},{10,8},{9,1... | collective-permute-start | bytes 3538952 | tf_op jit(solution)/shard_map/ppermute | solution.py:65
  96.4 21.4 %all-to-all-done.1 = bf16[6,256,256]{2,0,1:T(8,128)(2,1)S(1)} async-done(((bf16[6,256,256]{2,0,1:T(8,128)(2,1)}), bf16[6,256,256]{2,0,1:T(8,128)(2,1)S(1)}, u32[]{:S(2)}, u32[]{:S(2)}) %all-to-all-start.1) | async-done | bytes 786464 | tf_op jit(solution)/shard_map/all_to_all | solution.py:55
  119.6 1.5 collective-permute-start.1
  121.0 1.6 maximum_bitcast_fusion.2
  123.8 3.6 %fusion.105 = f32[192,1024]{1,0:T(8,128)S(1)} fusion(bf16[192,2048]{1,0:T(8,128)(2,1)} %bitcast.74, bf16[2048,1024]{1,0:T(8,128)(2,1)} %all-gather.2.cloned.1.call-done), kind=kOutput, calls=%fused_computation.230 | convolution fusion | flops 805306368 | bytes 5767168 | tf_op jit(solution)/shard_map/dot_general | solution.py:67
  127.5 2.3 %fusion.106 = f32[192,1024]{1,0:T(8,128)S(1)} fusion(bf16[192,2048]{1,0:T(8,128)(2,1)} %bitcast.17, bf16[2048,1024]{1,0:T(8,128)(2,1)S(1)} %copy-done.2), kind=kOutput, calls=%fused_computation.231 | convolution fusion | flops 805306368 | bytes 5767168 | tf_op jit(solution)/shard_map/dot_general | solution.py:67
  129.9 1.8 fusion.61
  132.6 1.9 collective-permute-start.7
  134.5 2.2 collective-permute-start.3
  136.7 1.3 collective-permute-start.2
  138.1 4.9 %collective-permute-start.5 = (f32[3,3,1,1024]{3,2,1,0:T(1,128)S(1)}, f32[3,3,1,1024]{3,2,1,0:T(1,128)S(1)}, u32[]{:S(2)}, u32[]{:S(2)}) collective-permute-start(f32[3,3,1,1024]{3,2,1,0:T(1,128)S(1)} %get-tuple-element.53), channel_id=1, source_target_pairs={{4,0},{8,4},{12,8},{16,12},{20,16},{24,20},{28,24},{5,1},{9,5},{13... | collective-permute-start | bytes 110600 | tf_op jit(solution)/shard_map/ppermute | solution.py:15
  143.0 1.9 collective-permute-start.4
  145.0 1.3 collective-permute-start.6
  146.4 1.8 collective-permute-done.6
  149.6 1.6 fusion.17
  153.0 2.4 %collective-permute-start.13 = (f32[3,3,32,1]{3,2,1,0:T(8,128)S(1)}, f32[3,3,32,1]{3,2,1,0:T(8,128)S(1)}, u32[]{:S(2)}, u32[]{:S(2)}) collective-permute-start(f32[3,3,32,1]{3,2,1,0:T(8,128)S(1)} %get-tuple-element.31), channel_id=1, source_target_pairs={{2,0},{3,1},{6,4},{7,5},{10,8},{11,9},{14,12},{15,13},{18,16},{19,... | collective-permute-start | bytes 3464 | tf_op jit(solution)/shard_map/ppermute | solution.py:15
  155.4 3.9 %collective-permute-start.9 = (f32[3,1,32,1024]{3,2,1,0:T(8,128)S(1)}, f32[3,1,32,1024]{3,2,1,0:T(8,128)S(1)}, u32[]{:S(2)}, u32[]{:S(2)}) collective-permute-start(f32[3,1,32,1024]{3,2,1,0:T(8,128)S(1)} %get-tuple-element.39), channel_id=1, source_target_pairs={{1,0},{3,2},{5,4},{7,6},{9,8},{11,10},{13,12},{15,14},{17,16},{19,... | collective-permute-start | bytes 1179656 | tf_op jit(solution)/shard_map/ppermute | solution.py:15
  159.3 1.3 collective-permute-start.8
  161.1 2.7 %collective-permute-start.11 = (f32[3,3,1,1024]{3,2,1,0:T(1,128)S(1)}, f32[3,3,1,1024]{3,2,1,0:T(1,128)S(1)}, u32[]{:S(2)}, u32[]{:S(2)}) collective-permute-start(f32[3,3,1,1024]{3,2,1,0:T(1,128)S(1)} %get-tuple-element.35), channel_id=1, source_target_pairs={{4,0},{8,4},{12,8},{16,12},{20,16},{24,20},{28,24},{5,1},{9,5},{13... | collective-permute-start | bytes 110600 | tf_op jit(solution)/shard_map/ppermute | solution.py:15
  163.8 2.6 %collective-permute-start.10 = (f32[3,3,1,1024]{3,2,1,0:T(1,128)S(1)}, f32[3,3,1,1024]{3,2,1,0:T(1,128)S(1)}, u32[]{:S(2)}, u32[]{:S(2)}) collective-permute-start(f32[3,3,1,1024]{3,2,1,0:T(1,128)S(1)} %get-tuple-element.36), channel_id=1, source_target_pairs={{0,4},{4,8},{8,12},{12,16},{16,20},{20,24},{24,28},{1,5},{5,9},{9,... | collective-permute-start | bytes 110600 | tf_op jit(solution)/shard_map/ppermute | solution.py:14
  166.4 1.5 collective-permute-start.12
  168.1 1.6 collective-permute-done.12
  169.7 2.5 %collective-permute-done.8 = f32[3,1,32,1024]{3,2,1,0:T(8,128)S(1)} collective-permute-done((f32[3,1,32,1024]{3,2,1,0:T(8,128)S(1)}, f32[3,1,32,1024]{3,2,1,0:T(8,128)S(1)}, u32[]{:S(2)}, u32[]{:S(2)}) %collective-permute-start.8) | collective-permute-done | bytes 393248 | tf_op jit(solution)/shard_map/ppermute | solution.py:14
  172.2 1.6 fusion.29
  174.5 2.4 %collective-permute-start.19 = (f32[3,3,32,1]{3,2,1,0:T(8,128)S(1)}, f32[3,3,32,1]{3,2,1,0:T(8,128)S(1)}, u32[]{:S(2)}, u32[]{:S(2)}) collective-permute-start(f32[3,3,32,1]{3,2,1,0:T(8,128)S(1)} %get-tuple-element.19), channel_id=1, source_target_pairs={{2,0},{3,1},{6,4},{7,5},{10,8},{11,9},{14,12},{15,13},{18,16},{19,... | collective-permute-start | bytes 3464 | tf_op jit(solution)/shard_map/ppermute | solution.py:15
  176.9 2.1 collective-permute-start.15
  180.8 2.7 %collective-permute-start.17 = (f32[3,3,1,1024]{3,2,1,0:T(1,128)S(1)}, f32[3,3,1,1024]{3,2,1,0:T(1,128)S(1)}, u32[]{:S(2)}, u32[]{:S(2)}) collective-permute-start(f32[3,3,1,1024]{3,2,1,0:T(1,128)S(1)} %get-tuple-element.23), channel_id=1, source_target_pairs={{4,0},{8,4},{12,8},{16,12},{20,16},{24,20},{28,24},{5,1},{9,5},{13... | collective-permute-start | bytes 110600 | tf_op jit(solution)/shard_map/ppermute | solution.py:15
  183.5 2.6 %collective-permute-start.16 = (f32[3,3,1,1024]{3,2,1,0:T(1,128)S(1)}, f32[3,3,1,1024]{3,2,1,0:T(1,128)S(1)}, u32[]{:S(2)}, u32[]{:S(2)}) collective-permute-start(f32[3,3,1,1024]{3,2,1,0:T(1,128)S(1)} %get-tuple-element.24), channel_id=1, source_target_pairs={{0,4},{4,8},{8,12},{12,16},{16,20},{20,24},{24,28},{1,5},{5,9},{9,... | collective-permute-start | bytes 110600 | tf_op jit(solution)/shard_map/ppermute | solution.py:14
  187.6 1.8 collective-permute-done.18
  189.4 2.5 %collective-permute-done.14 = f32[3,1,32,1024]{3,2,1,0:T(8,128)S(1)} collective-permute-done((f32[3,1,32,1024]{3,2,1,0:T(8,128)S(1)}, f32[3,1,32,1024]{3,2,1,0:T(8,128)S(1)}, u32[]{:S(2)}, u32[]{:S(2)}) %collective-permute-start.14) | collective-permute-done | bytes 393248 | tf_op jit(solution)/shard_map/ppermute | solution.py:14
  191.9 1.6 fusion.41
  194.2 2.4 %collective-permute-start.25 = (f32[3,3,32,1]{3,2,1,0:T(8,128)S(1)}, f32[3,3,32,1]{3,2,1,0:T(8,128)S(1)}, u32[]{:S(2)}, u32[]{:S(2)}) collective-permute-start(f32[3,3,32,1]{3,2,1,0:T(8,128)S(1)} %get-tuple-element.7), channel_id=1, source_target_pairs={{2,0},{3,1},{6,4},{7,5},{10,8},{11,9},{14,12},{15,13},{18,16},{19,... | collective-permute-start | bytes 3464 | tf_op jit(solution)/shard_map/ppermute | solution.py:15
  196.7 2.1 collective-permute-start.21
  200.6 2.7 %collective-permute-start.23 = (f32[3,3,1,1024]{3,2,1,0:T(1,128)S(1)}, f32[3,3,1,1024]{3,2,1,0:T(1,128)S(1)}, u32[]{:S(2)}, u32[]{:S(2)}) collective-permute-start(f32[3,3,1,1024]{3,2,1,0:T(1,128)S(1)} %get-tuple-element.11), channel_id=1, source_target_pairs={{4,0},{8,4},{12,8},{16,12},{20,16},{24,20},{28,24},{5,1},{9,5},{13... | collective-permute-start | bytes 110600 | tf_op jit(solution)/shard_map/ppermute | solution.py:15
  203.2 2.6 %collective-permute-start.22 = (f32[3,3,1,1024]{3,2,1,0:T(1,128)S(1)}, f32[3,3,1,1024]{3,2,1,0:T(1,128)S(1)}, u32[]{:S(2)}, u32[]{:S(2)}) collective-permute-start(f32[3,3,1,1024]{3,2,1,0:T(1,128)S(1)} %get-tuple-element.12), channel_id=1, source_target_pairs={{0,4},{4,8},{8,12},{12,16},{16,20},{20,24},{24,28},{1,5},{5,9},{9,... | collective-permute-start | bytes 110600 | tf_op jit(solution)/shard_map/ppermute | solution.py:14
  205.9 1.3 collective-permute-start.24
  207.4 1.8 collective-permute-done.24
  209.1 2.5 %collective-permute-done.20 = f32[3,1,32,1024]{3,2,1,0:T(8,128)S(1)} collective-permute-done((f32[3,1,32,1024]{3,2,1,0:T(8,128)S(1)}, f32[3,1,32,1024]{3,2,1,0:T(8,128)S(1)}, u32[]{:S(2)}, u32[]{:S(2)}) %collective-permute-start.20) | collective-permute-done | bytes 393248 | tf_op jit(solution)/shard_map/ppermute | solution.py:14
  211.7 1.6 fusion.53
  (81 shorter events, 19.7 us)
Async XLA Ops:
  6.5 1.2 copy-start
  6.5 2.1 copy-start.5
  6.5 117.3 %all-gather.2.cloned.1.call-start = ((), (), s32[]{:S(2)}) async-start(), calls=%async_computation.2 | async-start | bytes 4718592 | tf_op jit(solution)/shard_map/all_gather | solution.py:46
  18.6 5.8 %copy-start.6 = (bf16[32,256]{1,0:T(8,128)(2,1)S(1)}, bf16[32,256]{1,0:T(8,128)(2,1)}, u32[]{:S(2)}) copy-start(bf16[32,256]{1,0:T(8,128)(2,1)} %param.9) | copy-start | bytes 49156
  18.6 53.6 %all-to-all-start = ((bf16[8,2,24576]{2,1,0:T(2,128)(2,1)}), bf16[8,2,24576]{2,1,0:T(2,128)(2,1)S(1)}, u32[]{:S(2)}, u32[]{:S(2)}) async-start(bf16[8,2,24576]{2,1,0:T(2,128)(2,1)} %reshape.36), calls=%async_computation | async-start | bytes 1572864 | tf_op jit(solution)/shard_map/all_to_all | solution.py:52
  82.7 35.2 %all-to-all-start.1 = ((bf16[6,256,256]{2,0,1:T(8,128)(2,1)}), bf16[6,256,256]{2,0,1:T(8,128)(2,1)S(1)}, u32[]{:S(2)}, u32[]{:S(2)}) async-start(bf16[6,256,256]{2,0,1:T(8,128)(2,1)} %copy.31), calls=%async_computation.1 | async-start | bytes 2097152 | tf_op jit(solution)/shard_map/all_to_all | solution.py:55
  89.8 40.1 %collective-permute-start = (bf16[3,2,3,32,1024]{4,3,2,0,1:T(8,128)(2,1)}, bf16[3,2,3,32,1024]{4,3,2,0,1:T(8,128)(2,1)}, u32[]{:S(2)}, u32[]{:S(2)}) collective-permute-start(bf16[3,2,3,32,1024]{4,3,2,0,1:T(8,128)(2,1)} %copy.44), channel_id=1, source_target_pairs={{0,2},{2,0},{1,3},{3,1},{4,6},{6,4},{5,7},{7,5},{8,10},{10,8},{9,1... | collective-permute-start | bytes 3538952 | tf_op jit(solution)/shard_map/ppermute | solution.py:65
  119.6 7.9 %collective-permute-start.1 = (bf16[6,32,2048]{2,1,0:T(8,128)(2,1)}, bf16[6,32,2048]{2,1,0:T(8,128)(2,1)}, u32[]{:S(2)}, u32[]{:S(2)}) collective-permute-start(bf16[6,32,2048]{2,1,0:T(8,128)(2,1)} %all_to_all.33), channel_id=1, source_target_pairs={{0,2},{2,0},{1,3},{3,1},{4,6},{6,4},{5,7},{7,5},{8,10},{10,8},{9,1... | collective-permute-start | bytes 2359304 | tf_op jit(solution)/shard_map/ppermute | solution.py:66
  123.8 3.7 %copy-start.2 = (bf16[2048,1024]{1,0:T(8,128)(2,1)S(1)}, bf16[2048,1024]{1,0:T(8,128)(2,1)}, u32[]{:S(2)}) copy-start(bf16[2048,1024]{1,0:T(8,128)(2,1)} %all-gather.2.cloned.1.call-done) | copy-start | bytes 12582916
  127.5 2.4 %copy-start.4 = (bf16[3,2,3,32,2048]{4,3,2,1,0:T(8,128)(2,1)S(1)}, bf16[3,2,3,32,2048]{4,3,2,1,0:T(8,128)(2,1)}, u32[]{:S(2)}) copy-start(bf16[3,2,3,32,2048]{4,3,2,1,0:T(8,128)(2,1)} %param.7) | copy-start | bytes 7077892
  132.6 12.4 %collective-permute-start.7 = (f32[3,3,32,1]{3,2,1,0:T(8,128)S(1)}, f32[3,3,32,1]{3,2,1,0:T(8,128)S(1)}, u32[]{:S(2)}, u32[]{:S(2)}) collective-permute-start(f32[3,3,32,1]{3,2,1,0:T(8,128)S(1)} %get-tuple-element.49), channel_id=1, source_target_pairs={{2,0},{3,1},{6,4},{7,5},{10,8},{11,9},{14,12},{15,13},{18,16},{19,... | collective-permute-start | bytes 3464 | tf_op jit(solution)/shard_map/ppermute | solution.py:15
  134.5 14.1 %collective-permute-start.3 = (f32[3,1,32,1024]{3,2,1,0:T(8,128)S(1)}, f32[3,1,32,1024]{3,2,1,0:T(8,128)S(1)}, u32[]{:S(2)}, u32[]{:S(2)}) collective-permute-start(f32[3,1,32,1024]{3,2,1,0:T(8,128)S(1)} %get-tuple-element.57), channel_id=1, source_target_pairs={{1,0},{3,2},{5,4},{7,6},{9,8},{11,10},{13,12},{15,14},{17,16},{19,... | collective-permute-start | bytes 1179656 | tf_op jit(solution)/shard_map/ppermute | solution.py:15
  136.7 12.9 %collective-permute-start.2 = (f32[3,1,32,1024]{3,2,1,0:T(8,128)S(1)}, f32[3,1,32,1024]{3,2,1,0:T(8,128)S(1)}, u32[]{:S(2)}, u32[]{:S(2)}) collective-permute-start(f32[3,1,32,1024]{3,2,1,0:T(8,128)S(1)} %get-tuple-element.58), channel_id=1, source_target_pairs={{0,1},{2,3},{4,5},{6,7},{8,9},{10,11},{12,13},{14,15},{16,17},{18,... | collective-permute-start | bytes 1179656 | tf_op jit(solution)/shard_map/ppermute | solution.py:14
  138.1 10.1 %collective-permute-start.5 = (f32[3,3,1,1024]{3,2,1,0:T(1,128)S(1)}, f32[3,3,1,1024]{3,2,1,0:T(1,128)S(1)}, u32[]{:S(2)}, u32[]{:S(2)}) collective-permute-start(f32[3,3,1,1024]{3,2,1,0:T(1,128)S(1)} %get-tuple-element.53), channel_id=1, source_target_pairs={{4,0},{8,4},{12,8},{16,12},{20,16},{24,20},{28,24},{5,1},{9,5},{13... | collective-permute-start | bytes 110600 | tf_op jit(solution)/shard_map/ppermute | solution.py:15
  143.0 5.6 %collective-permute-start.4 = (f32[3,3,1,1024]{3,2,1,0:T(1,128)S(1)}, f32[3,3,1,1024]{3,2,1,0:T(1,128)S(1)}, u32[]{:S(2)}, u32[]{:S(2)}) collective-permute-start(f32[3,3,1,1024]{3,2,1,0:T(1,128)S(1)} %get-tuple-element.54), channel_id=1, source_target_pairs={{0,4},{4,8},{8,12},{12,16},{16,20},{20,24},{24,28},{1,5},{5,9},{9,... | collective-permute-start | bytes 110600 | tf_op jit(solution)/shard_map/ppermute | solution.py:14
  145.0 3.3 %collective-permute-start.6 = (f32[3,3,32,1]{3,2,1,0:T(8,128)S(1)}, f32[3,3,32,1]{3,2,1,0:T(8,128)S(1)}, u32[]{:S(2)}, u32[]{:S(2)}) collective-permute-start(f32[3,3,32,1]{3,2,1,0:T(8,128)S(1)} %get-tuple-element.50), channel_id=1, source_target_pairs={{0,2},{1,3},{4,6},{5,7},{8,10},{9,11},{12,14},{13,15},{16,18},{17,... | collective-permute-start | bytes 3464 | tf_op jit(solution)/shard_map/ppermute | solution.py:14
  151.2 1.1 copy-start.3
  153.0 13.4 %collective-permute-start.13 = (f32[3,3,32,1]{3,2,1,0:T(8,128)S(1)}, f32[3,3,32,1]{3,2,1,0:T(8,128)S(1)}, u32[]{:S(2)}, u32[]{:S(2)}) collective-permute-start(f32[3,3,32,1]{3,2,1,0:T(8,128)S(1)} %get-tuple-element.31), channel_id=1, source_target_pairs={{2,0},{3,1},{6,4},{7,5},{10,8},{11,9},{14,12},{15,13},{18,16},{19,... | collective-permute-start | bytes 3464 | tf_op jit(solution)/shard_map/ppermute | solution.py:15
  155.4 14.3 %collective-permute-start.9 = (f32[3,1,32,1024]{3,2,1,0:T(8,128)S(1)}, f32[3,1,32,1024]{3,2,1,0:T(8,128)S(1)}, u32[]{:S(2)}, u32[]{:S(2)}) collective-permute-start(f32[3,1,32,1024]{3,2,1,0:T(8,128)S(1)} %get-tuple-element.39), channel_id=1, source_target_pairs={{1,0},{3,2},{5,4},{7,6},{9,8},{11,10},{13,12},{15,14},{17,16},{19,... | collective-permute-start | bytes 1179656 | tf_op jit(solution)/shard_map/ppermute | solution.py:15
  159.3 12.9 %collective-permute-start.8 = (f32[3,1,32,1024]{3,2,1,0:T(8,128)S(1)}, f32[3,1,32,1024]{3,2,1,0:T(8,128)S(1)}, u32[]{:S(2)}, u32[]{:S(2)}) collective-permute-start(f32[3,1,32,1024]{3,2,1,0:T(8,128)S(1)} %get-tuple-element.40), channel_id=1, source_target_pairs={{0,1},{2,3},{4,5},{6,7},{8,9},{10,11},{12,13},{14,15},{16,17},{18,... | collective-permute-start | bytes 1179656 | tf_op jit(solution)/shard_map/ppermute | solution.py:14
  161.1 8.6 %collective-permute-start.11 = (f32[3,3,1,1024]{3,2,1,0:T(1,128)S(1)}, f32[3,3,1,1024]{3,2,1,0:T(1,128)S(1)}, u32[]{:S(2)}, u32[]{:S(2)}) collective-permute-start(f32[3,3,1,1024]{3,2,1,0:T(1,128)S(1)} %get-tuple-element.35), channel_id=1, source_target_pairs={{4,0},{8,4},{12,8},{16,12},{20,16},{24,20},{28,24},{5,1},{9,5},{13... | collective-permute-start | bytes 110600 | tf_op jit(solution)/shard_map/ppermute | solution.py:15
  163.8 5.9 %collective-permute-start.10 = (f32[3,3,1,1024]{3,2,1,0:T(1,128)S(1)}, f32[3,3,1,1024]{3,2,1,0:T(1,128)S(1)}, u32[]{:S(2)}, u32[]{:S(2)}) collective-permute-start(f32[3,3,1,1024]{3,2,1,0:T(1,128)S(1)} %get-tuple-element.36), channel_id=1, source_target_pairs={{0,4},{4,8},{8,12},{12,16},{16,20},{20,24},{24,28},{1,5},{5,9},{9,... | collective-permute-start | bytes 110600 | tf_op jit(solution)/shard_map/ppermute | solution.py:14
  166.4 3.3 %collective-permute-start.12 = (f32[3,3,32,1]{3,2,1,0:T(8,128)S(1)}, f32[3,3,32,1]{3,2,1,0:T(8,128)S(1)}, u32[]{:S(2)}, u32[]{:S(2)}) collective-permute-start(f32[3,3,32,1]{3,2,1,0:T(8,128)S(1)} %get-tuple-element.32), channel_id=1, source_target_pairs={{0,2},{1,3},{4,6},{5,7},{8,10},{9,11},{12,14},{13,15},{16,18},{17,... | collective-permute-start | bytes 3464 | tf_op jit(solution)/shard_map/ppermute | solution.py:14
  174.5 11.6 %collective-permute-start.19 = (f32[3,3,32,1]{3,2,1,0:T(8,128)S(1)}, f32[3,3,32,1]{3,2,1,0:T(8,128)S(1)}, u32[]{:S(2)}, u32[]{:S(2)}) collective-permute-start(f32[3,3,32,1]{3,2,1,0:T(8,128)S(1)} %get-tuple-element.19), channel_id=1, source_target_pairs={{2,0},{3,1},{6,4},{7,5},{10,8},{11,9},{14,12},{15,13},{18,16},{19,... | collective-permute-start | bytes 3464 | tf_op jit(solution)/shard_map/ppermute | solution.py:15
  176.9 12.5 %collective-permute-start.15 = (f32[3,1,32,1024]{3,2,1,0:T(8,128)S(1)}, f32[3,1,32,1024]{3,2,1,0:T(8,128)S(1)}, u32[]{:S(2)}, u32[]{:S(2)}) collective-permute-start(f32[3,1,32,1024]{3,2,1,0:T(8,128)S(1)} %get-tuple-element.27), channel_id=1, source_target_pairs={{1,0},{3,2},{5,4},{7,6},{9,8},{11,10},{13,12},{15,14},{17,16},{19,... | collective-permute-start | bytes 1179656 | tf_op jit(solution)/shard_map/ppermute | solution.py:15
  179.0 12.9 %collective-permute-start.14 = (f32[3,1,32,1024]{3,2,1,0:T(8,128)S(1)}, f32[3,1,32,1024]{3,2,1,0:T(8,128)S(1)}, u32[]{:S(2)}, u32[]{:S(2)}) collective-permute-start(f32[3,1,32,1024]{3,2,1,0:T(8,128)S(1)} %get-tuple-element.28), channel_id=1, source_target_pairs={{0,1},{2,3},{4,5},{6,7},{8,9},{10,11},{12,13},{14,15},{16,17},{18,... | collective-permute-start | bytes 1179656 | tf_op jit(solution)/shard_map/ppermute | solution.py:14
  180.8 8.6 %collective-permute-start.17 = (f32[3,3,1,1024]{3,2,1,0:T(1,128)S(1)}, f32[3,3,1,1024]{3,2,1,0:T(1,128)S(1)}, u32[]{:S(2)}, u32[]{:S(2)}) collective-permute-start(f32[3,3,1,1024]{3,2,1,0:T(1,128)S(1)} %get-tuple-element.23), channel_id=1, source_target_pairs={{4,0},{8,4},{12,8},{16,12},{20,16},{24,20},{28,24},{5,1},{9,5},{13... | collective-permute-start | bytes 110600 | tf_op jit(solution)/shard_map/ppermute | solution.py:15
  183.5 5.9 %collective-permute-start.16 = (f32[3,3,1,1024]{3,2,1,0:T(1,128)S(1)}, f32[3,3,1,1024]{3,2,1,0:T(1,128)S(1)}, u32[]{:S(2)}, u32[]{:S(2)}) collective-permute-start(f32[3,3,1,1024]{3,2,1,0:T(1,128)S(1)} %get-tuple-element.24), channel_id=1, source_target_pairs={{0,4},{4,8},{8,12},{12,16},{16,20},{20,24},{24,28},{1,5},{5,9},{9,... | collective-permute-start | bytes 110600 | tf_op jit(solution)/shard_map/ppermute | solution.py:14
  186.1 3.3 %collective-permute-start.18 = (f32[3,3,32,1]{3,2,1,0:T(8,128)S(1)}, f32[3,3,32,1]{3,2,1,0:T(8,128)S(1)}, u32[]{:S(2)}, u32[]{:S(2)}) collective-permute-start(f32[3,3,32,1]{3,2,1,0:T(8,128)S(1)} %get-tuple-element.20), channel_id=1, source_target_pairs={{0,2},{1,3},{4,6},{5,7},{8,10},{9,11},{12,14},{13,15},{16,18},{17,... | collective-permute-start | bytes 3464 | tf_op jit(solution)/shard_map/ppermute | solution.py:14
  194.2 11.6 %collective-permute-start.25 = (f32[3,3,32,1]{3,2,1,0:T(8,128)S(1)}, f32[3,3,32,1]{3,2,1,0:T(8,128)S(1)}, u32[]{:S(2)}, u32[]{:S(2)}) collective-permute-start(f32[3,3,32,1]{3,2,1,0:T(8,128)S(1)} %get-tuple-element.7), channel_id=1, source_target_pairs={{2,0},{3,1},{6,4},{7,5},{10,8},{11,9},{14,12},{15,13},{18,16},{19,... | collective-permute-start | bytes 3464 | tf_op jit(solution)/shard_map/ppermute | solution.py:15
  196.7 12.5 %collective-permute-start.21 = (f32[3,1,32,1024]{3,2,1,0:T(8,128)S(1)}, f32[3,1,32,1024]{3,2,1,0:T(8,128)S(1)}, u32[]{:S(2)}, u32[]{:S(2)}) collective-permute-start(f32[3,1,32,1024]{3,2,1,0:T(8,128)S(1)} %get-tuple-element.15), channel_id=1, source_target_pairs={{1,0},{3,2},{5,4},{7,6},{9,8},{11,10},{13,12},{15,14},{17,16},{19,... | collective-permute-start | bytes 1179656 | tf_op jit(solution)/shard_map/ppermute | solution.py:15
  198.7 12.9 %collective-permute-start.20 = (f32[3,1,32,1024]{3,2,1,0:T(8,128)S(1)}, f32[3,1,32,1024]{3,2,1,0:T(8,128)S(1)}, u32[]{:S(2)}, u32[]{:S(2)}) collective-permute-start(f32[3,1,32,1024]{3,2,1,0:T(8,128)S(1)} %get-tuple-element.16), channel_id=1, source_target_pairs={{0,1},{2,3},{4,5},{6,7},{8,9},{10,11},{12,13},{14,15},{16,17},{18,... | collective-permute-start | bytes 1179656 | tf_op jit(solution)/shard_map/ppermute | solution.py:14
  200.6 8.6 %collective-permute-start.23 = (f32[3,3,1,1024]{3,2,1,0:T(1,128)S(1)}, f32[3,3,1,1024]{3,2,1,0:T(1,128)S(1)}, u32[]{:S(2)}, u32[]{:S(2)}) collective-permute-start(f32[3,3,1,1024]{3,2,1,0:T(1,128)S(1)} %get-tuple-element.11), channel_id=1, source_target_pairs={{4,0},{8,4},{12,8},{16,12},{20,16},{24,20},{28,24},{5,1},{9,5},{13... | collective-permute-start | bytes 110600 | tf_op jit(solution)/shard_map/ppermute | solution.py:15
  203.2 5.9 %collective-permute-start.22 = (f32[3,3,1,1024]{3,2,1,0:T(1,128)S(1)}, f32[3,3,1,1024]{3,2,1,0:T(1,128)S(1)}, u32[]{:S(2)}, u32[]{:S(2)}) collective-permute-start(f32[3,3,1,1024]{3,2,1,0:T(1,128)S(1)} %get-tuple-element.12), channel_id=1, source_target_pairs={{0,4},{4,8},{8,12},{12,16},{16,20},{20,24},{24,28},{1,5},{5,9},{9,... | collective-permute-start | bytes 110600 | tf_op jit(solution)/shard_map/ppermute | solution.py:14
  205.9 3.3 %collective-permute-start.24 = (f32[3,3,32,1]{3,2,1,0:T(8,128)S(1)}, f32[3,3,32,1]{3,2,1,0:T(8,128)S(1)}, u32[]{:S(2)}, u32[]{:S(2)}) collective-permute-start(f32[3,3,32,1]{3,2,1,0:T(8,128)S(1)} %get-tuple-element.8), channel_id=1, source_target_pairs={{0,2},{1,3},{4,6},{5,7},{8,10},{9,11},{12,14},{13,15},{16,18},{17,... | collective-permute-start | bytes 3464 | tf_op jit(solution)/shard_map/ppermute | solution.py:14
  213.4 1.4 copy-start.1
Sparse Core Ops, SparseCore 0:
  9.5 94.2 all-gather.1
where the time goes:
time: 223 us; the launch traced here: 222 us
  starting transfers between devices  71.2 us (32%)
  blocking collectives  47.8 us (21%)
  waiting for transfers between devices  37.3 us (17%)
  local copies, waits for them, and re-layouts  30.3 us (14%)
  other arithmetic  14.8 us (7%)
  between operations  14 us (6%)
  matrix products  6.28 us (3%)
    all_gather x1, blocking collectives, on_device(): row_whole = lax.all_gather(row_taper, 'row', axis=0, tiled=True)  47.8 us
    ppermute x12, starting transfers between devices, faces(): high = lax.ppermute(lax.slice_in_dim(block, 0, 1, axis=dim), axis, backward)  32.5 us
    all_to_all x1, waiting for transfers between devices, on_device(): lax.all_to_all(tapered.astype(jnp.bfloat16), 'row', split_axis=1, concat_...  21.4 us
    ppermute x12, starting transfers between devices, faces(): lax.ppermute(lax.slice_in_dim(block, last - 1, last, axis=dim), axis, for...  20.2 us
    ppermute x12, waiting for transfers between devices, faces(): lax.ppermute(lax.slice_in_dim(block, last - 1, last, axis=dim), axis, for...  15.8 us
    unnamed x18, local copies, waits for them, and re-layouts  14.7 us
    ppermute x1, starting transfers between devices, on_device(): part = lax.ppermute(part, 'mem', ring)  6.65 us
    sub x4, other arithmetic, advance(): shifted = present - change  6.37 us
  transfers between devices with their start and end apart: 29, of which 10 were waited for; matrix products, arithmetic and copies ran while one was open for 16% of the time, Pallas kernels for 0%

commit v1 on v0

--- a/solution.py
+++ b/solution.py
@@ -52,9 +52,11 @@
         lax.all_to_all(fields, "row", split_axis=2, concat_axis=1, tiled=True),
         preferred_element_type=jnp.float32,
     )
-    tapered = lax.all_to_all(
-        tapered.astype(jnp.bfloat16), "row", split_axis=1, concat_axis=2, tiled=True
-    )
+    part_2 = tapered.astype(jnp.bfloat16)
+    count_2 = lax.axis_size("row")
+    blocks = jnp.stack(jnp.split(part_2, count_2, axis=1), axis=0)
+    blocks = lax.all_to_all(blocks, "row", split_axis=0, concat_axis=0)
+    tapered = jnp.concatenate(blocks, axis=2)
     weighted = 0.0
     for shift in range(mem_count):
         ring = [(i, (i + shift) % mem_count) for i in range(mem_count)]

time: 223 us -> 216 us (0.969)
  waiting for transfers between devices: 37.3 us -> 30.4 us
    all_to_all x1, waiting for transfers between devices: 21.4 us -> 13.7 us  [on_device(): blocks = lax.all_to_all(blocks, 'row', split_axis=0, concat_axis=0)]
    unnamed x18 -> x27, local copies, waits for them, and re-layouts: 14.7 us -> 18.2 us
  transfers between devices with their start and end apart: 29 -> 29, of which waited for: 10 -> 10; matrix products, arithmetic and copies ran while one was open for 16% -> 17% of each run, Pallas kernels for 0% -> 0%
where the time goes in v1:
time: 216 us; the launch traced here: 215 us
  starting transfers between devices  70.5 us (33%)
  blocking collectives  47.8 us (22%)
  local copies, waits for them, and re-layouts  31.1 us (14%)
  waiting for transfers between devices  30.4 us (14%)
  other arithmetic  14.8 us (7%)
  between operations  14.1 us (7%)
  matrix products  6 us (3%)
    all_gather x1, blocking collectives, on_device(): row_whole = lax.all_gather(row_taper, 'row', axis=0, tiled=True)  47.8 us
    ppermute x12, starting transfers between devices, faces(): high = lax.ppermute(lax.slice_in_dim(block, 0, 1, axis=dim), axis, backward)  30.9 us
    ppermute x12, starting transfers between devices, faces(): lax.ppermute(lax.slice_in_dim(block, last - 1, last, axis=dim), axis, for...  20.2 us
    unnamed x27, local copies, waits for them, and re-layouts  18.2 us
    ppermute x12, waiting for transfers between devices, faces(): lax.ppermute(lax.slice_in_dim(block, last - 1, last, axis=dim), axis, for...  16.6 us
    all_to_all x1, waiting for transfers between devices, on_device(): blocks = lax.all_to_all(blocks, 'row', split_axis=0, concat_axis=0)  13.7 us
    ppermute x1, starting transfers between devices, on_device(): part = lax.ppermute(part, 'mem', ring)  6.67 us
    sub x4, other arithmetic, advance(): shifted = present - change  6.37 us
  transfers between devices with their start and end apart: 29, of which 10 were waited for; matrix products, arithmetic and copies ran while one was open for 17% of the time, Pallas kernels for 0%

profile of v1, /device:TPU:13, one launch (start us, length us, event | category | flops | bytes accessed | tf_op | source)
XLA Modules:
  0.0 214.6 jit_solution(9838749976002999155)
XLA Ops:
  8.6 4.2 %copy.22 = bf16[6,32,2048]{1,0,2:T(8,128)(2,1)} copy(bf16[6,32,2048]{2,1,0:T(8,128)(2,1)S(1)} %bitcast.108) | data formatting | bytes 1572864 | tf_op jit(solution)/shard_map/reshape | solution.py:48
  12.9 5.7 %reshape.39 = bf16[8,2,24576]{2,1,0:T(2,128)(2,1)} reshape(bf16[2048,6,32]{2,1,0:T(8,128)(2,1)} %bitcast.98) | data formatting | bytes 1572864
  18.6 5.8 %all-to-all-start = ((bf16[8,2,24576]{2,1,0:T(2,128)(2,1)}), bf16[8,2,24576]{2,1,0:T(2,128)(2,1)S(1)}, u32[]{:S(2)}, u32[]{:S(2)}) async-start(bf16[8,2,24576]{2,1,0:T(2,128)(2,1)} %reshape.39), calls=%async_computation | async-start | bytes 1572864 | tf_op jit(solution)/shard_map/all_to_all | solution.py:52
  24.4 47.8 %all_gather.6 = bf16[256,256]{1,0:T(8,128)(2,1)S(1)} all-gather(bf16[32,256]{1,0:T(8,128)(2,1)S(1)} %copy-done.7), channel_id=1, replica_groups=mesh['row'=8,'mem'=2,'lev'=2] {'row'}, dimensions={0}, use_global_device_ids=true | all-gather | bytes 147456 | tf_op jit(solution)/shard_map/all_gather | solution.py:47
  72.2 4.2 %reshape.40 = bf16[2048,6,32]{2,1,0:T(8,128)(2,1)} reshape(bf16[8,2,24576]{2,1,0:T(2,128)(2,1)S(1)} %all-to-all-done) | data formatting | bytes 1572864
  76.4 4.1 %copy.24 = bf16[6,8,32,256]{3,2,1,0:T(8,128)(2,1)S(1)} copy(bf16[6,8,32,256]{2,0,3,1:T(8,128)(2,1)} %bitcast.97) | data formatting | bytes 1572864 | tf_op jit(solution)/shard_map/all_to_all | solution.py:52
  86.0 4.5 %all-to-all-start.1 = ((bf16[8,6,32,256]{3,2,1,0:T(8,128)(2,1)}), bf16[8,6,32,256]{3,2,1,0:T(8,128)(2,1)S(1)}, u32[]{:S(2)}, u32[]{:S(2)}) async-start(bf16[8,6,32,256]{3,2,1,0:T(8,128)(2,1)} %fusion.91), calls=%async_computation.1 | async-start | bytes 1572864 | tf_op jit(solution)/shard_map/all_to_all | solution.py:58
  91.8 6.7 %collective-permute-start = (bf16[3,2,3,32,1024]{4,3,2,0,1:T(8,128)(2,1)}, bf16[3,2,3,32,1024]{4,3,2,0,1:T(8,128)(2,1)}, u32[]{:S(2)}, u32[]{:S(2)}) collective-permute-start(bf16[3,2,3,32,1024]{4,3,2,0,1:T(8,128)(2,1)} %copy.33), channel_id=1, source_target_pairs={{0,2},{2,0},{1,3},{3,1},{4,6},{6,4},{5,7},{7,5},{8,10},{10,8},{9,1... | collective-permute-start | bytes 3538952 | tf_op jit(solution)/shard_map/ppermute | solution.py:67
  98.5 13.7 %all-to-all-done.1 = bf16[8,6,32,256]{3,2,1,0:T(8,128)(2,1)S(1)} async-done(((bf16[8,6,32,256]{3,2,1,0:T(8,128)(2,1)}), bf16[8,6,32,256]{3,2,1,0:T(8,128)(2,1)S(1)}, u32[]{:S(2)}, u32[]{:S(2)}) %all-to-all-start.1) | async-done | bytes 786464 | tf_op jit(solution)/shard_map/all_to_all | solution.py:58
  113.2 2.3 %collective-permute-start.1 = (bf16[6,32,2048]{2,1,0:T(8,128)(2,1)}, bf16[6,32,2048]{2,1,0:T(8,128)(2,1)}, u32[]{:S(2)}, u32[]{:S(2)}) collective-permute-start(bf16[6,32,2048]{2,1,0:T(8,128)(2,1)} %bitcast.41), channel_id=1, source_target_pairs={{0,2},{2,0},{1,3},{3,1},{4,6},{6,4},{5,7},{7,5},{8,10},{10,8},{9,1... | collective-permute-start | bytes 2359304 | tf_op jit(solution)/shard_map/ppermute | solution.py:68
  115.5 1.6 maximum_bitcast_fusion.2
  117.8 3.3 %fusion.113 = f32[192,1024]{1,0:T(8,128)S(1)} fusion(bf16[192,2048]{1,0:T(8,128)(2,1)S(1)} %bitcast.103, bf16[2048,1024]{1,0:T(8,128)(2,1)} %all-gather.2.cloned.1.call-done), kind=kOutput, calls=%fused_computation.246 | convolution fusion | flops 805306368 | bytes 5767168 | tf_op jit(solution)/shard_map/dot_general | solution.py:69
  121.2 2.3 %fusion.114 = f32[192,1024]{1,0:T(8,128)S(1)} fusion(bf16[192,2048]{1,0:T(8,128)(2,1)} %bitcast.21, bf16[2048,1024]{1,0:T(8,128)(2,1)S(1)} %copy-done.2), kind=kOutput, calls=%fused_computation.247 | convolution fusion | flops 805306368 | bytes 5767168 | tf_op jit(solution)/shard_map/dot_general | solution.py:69
  123.6 1.8 fusion.61
  126.3 1.9 collective-permute-start.7
  128.2 2.2 %collective-permute-start.3 = (f32[3,1,32,1024]{3,2,1,0:T(8,128)S(1)}, f32[3,1,32,1024]{3,2,1,0:T(8,128)S(1)}, u32[]{:S(2)}, u32[]{:S(2)}) collective-permute-start(f32[3,1,32,1024]{3,2,1,0:T(8,128)S(1)} %get-tuple-element.57), channel_id=1, source_target_pairs={{1,0},{3,2},{5,4},{7,6},{9,8},{11,10},{13,12},{15,14},{17,16},{19,... | collective-permute-start | bytes 1179656 | tf_op jit(solution)/shard_map/ppermute | solution.py:15
  130.4 1.3 collective-permute-start.2
  131.8 4.2 %collective-permute-start.5 = (f32[3,3,1,1024]{3,2,1,0:T(1,128)S(1)}, f32[3,3,1,1024]{3,2,1,0:T(1,128)S(1)}, u32[]{:S(2)}, u32[]{:S(2)}) collective-permute-start(f32[3,3,1,1024]{3,2,1,0:T(1,128)S(1)} %get-tuple-element.53), channel_id=1, source_target_pairs={{4,0},{8,4},{12,8},{16,12},{20,16},{24,20},{28,24},{5,1},{9,5},{13... | collective-permute-start | bytes 110600 | tf_op jit(solution)/shard_map/ppermute | solution.py:15
  136.0 1.9 collective-permute-start.4
  137.9 1.3 collective-permute-start.6
  139.4 1.8 collective-permute-done.6
  141.6 1.8 collective-permute-done.2
  143.4 1.6 fusion.17
  146.7 2.4 %collective-permute-start.13 = (f32[3,3,32,1]{3,2,1,0:T(8,128)S(1)}, f32[3,3,32,1]{3,2,1,0:T(8,128)S(1)}, u32[]{:S(2)}, u32[]{:S(2)}) collective-permute-start(f32[3,3,32,1]{3,2,1,0:T(8,128)S(1)} %get-tuple-element.31), channel_id=1, source_target_pairs={{2,0},{3,1},{6,4},{7,5},{10,8},{11,9},{14,12},{15,13},{18,16},{19,... | collective-permute-start | bytes 3464 | tf_op jit(solution)/shard_map/ppermute | solution.py:15
  149.1 3.1 %collective-permute-start.9 = (f32[3,1,32,1024]{3,2,1,0:T(8,128)S(1)}, f32[3,1,32,1024]{3,2,1,0:T(8,128)S(1)}, u32[]{:S(2)}, u32[]{:S(2)}) collective-permute-start(f32[3,1,32,1024]{3,2,1,0:T(8,128)S(1)} %get-tuple-element.39), channel_id=1, source_target_pairs={{1,0},{3,2},{5,4},{7,6},{9,8},{11,10},{13,12},{15,14},{17,16},{19,... | collective-permute-start | bytes 1179656 | tf_op jit(solution)/shard_map/ppermute | solution.py:15
  152.3 1.3 collective-permute-start.8
  154.1 2.7 %collective-permute-start.11 = (f32[3,3,1,1024]{3,2,1,0:T(1,128)S(1)}, f32[3,3,1,1024]{3,2,1,0:T(1,128)S(1)}, u32[]{:S(2)}, u32[]{:S(2)}) collective-permute-start(f32[3,3,1,1024]{3,2,1,0:T(1,128)S(1)} %get-tuple-element.35), channel_id=1, source_target_pairs={{4,0},{8,4},{12,8},{16,12},{20,16},{24,20},{28,24},{5,1},{9,5},{13... | collective-permute-start | bytes 110600 | tf_op jit(solution)/shard_map/ppermute | solution.py:15
  156.8 2.6 %collective-permute-start.10 = (f32[3,3,1,1024]{3,2,1,0:T(1,128)S(1)}, f32[3,3,1,1024]{3,2,1,0:T(1,128)S(1)}, u32[]{:S(2)}, u32[]{:S(2)}) collective-permute-start(f32[3,3,1,1024]{3,2,1,0:T(1,128)S(1)} %get-tuple-element.36), channel_id=1, source_target_pairs={{0,4},{4,8},{8,12},{12,16},{16,20},{20,24},{24,28},{1,5},{5,9},{9,... | collective-permute-start | bytes 110600 | tf_op jit(solution)/shard_map/ppermute | solution.py:14
  159.4 1.5 collective-permute-start.12
  161.1 1.6 collective-permute-done.12
  162.6 2.5 %collective-permute-done.8 = f32[3,1,32,1024]{3,2,1,0:T(8,128)S(1)} collective-permute-done((f32[3,1,32,1024]{3,2,1,0:T(8,128)S(1)}, f32[3,1,32,1024]{3,2,1,0:T(8,128)S(1)}, u32[]{:S(2)}, u32[]{:S(2)}) %collective-permute-start.8) | collective-permute-done | bytes 393248 | tf_op jit(solution)/shard_map/ppermute | solution.py:14
  165.2 1.6 fusion.29
  167.5 2.4 %collective-permute-start.19 = (f32[3,3,32,1]{3,2,1,0:T(8,128)S(1)}, f32[3,3,32,1]{3,2,1,0:T(8,128)S(1)}, u32[]{:S(2)}, u32[]{:S(2)}) collective-permute-start(f32[3,3,32,1]{3,2,1,0:T(8,128)S(1)} %get-tuple-element.19), channel_id=1, source_target_pairs={{2,0},{3,1},{6,4},{7,5},{10,8},{11,9},{14,12},{15,13},{18,16},{19,... | collective-permute-start | bytes 3464 | tf_op jit(solution)/shard_map/ppermute | solution.py:15
  169.9 2.1 collective-permute-start.15
  172.0 1.3 collective-permute-start.14
  173.8 2.7 %collective-permute-start.17 = (f32[3,3,1,1024]{3,2,1,0:T(1,128)S(1)}, f32[3,3,1,1024]{3,2,1,0:T(1,128)S(1)}, u32[]{:S(2)}, u32[]{:S(2)}) collective-permute-start(f32[3,3,1,1024]{3,2,1,0:T(1,128)S(1)} %get-tuple-element.23), channel_id=1, source_target_pairs={{4,0},{8,4},{12,8},{16,12},{20,16},{24,20},{28,24},{5,1},{9,5},{13... | collective-permute-start | bytes 110600 | tf_op jit(solution)/shard_map/ppermute | solution.py:15
  176.5 2.6 %collective-permute-start.16 = (f32[3,3,1,1024]{3,2,1,0:T(1,128)S(1)}, f32[3,3,1,1024]{3,2,1,0:T(1,128)S(1)}, u32[]{:S(2)}, u32[]{:S(2)}) collective-permute-start(f32[3,3,1,1024]{3,2,1,0:T(1,128)S(1)} %get-tuple-element.24), channel_id=1, source_target_pairs={{0,4},{4,8},{8,12},{12,16},{16,20},{20,24},{24,28},{1,5},{5,9},{9,... | collective-permute-start | bytes 110600 | tf_op jit(solution)/shard_map/ppermute | solution.py:14
  180.6 1.8 collective-permute-done.18
  182.4 2.5 %collective-permute-done.14 = f32[3,1,32,1024]{3,2,1,0:T(8,128)S(1)} collective-permute-done((f32[3,1,32,1024]{3,2,1,0:T(8,128)S(1)}, f32[3,1,32,1024]{3,2,1,0:T(8,128)S(1)}, u32[]{:S(2)}, u32[]{:S(2)}) %collective-permute-start.14) | collective-permute-done | bytes 393248 | tf_op jit(solution)/shard_map/ppermute | solution.py:14
  184.9 1.6 fusion.41
  187.2 2.4 %collective-permute-start.25 = (f32[3,3,32,1]{3,2,1,0:T(8,128)S(1)}, f32[3,3,32,1]{3,2,1,0:T(8,128)S(1)}, u32[]{:S(2)}, u32[]{:S(2)}) collective-permute-start(f32[3,3,32,1]{3,2,1,0:T(8,128)S(1)} %get-tuple-element.7), channel_id=1, source_target_pairs={{2,0},{3,1},{6,4},{7,5},{10,8},{11,9},{14,12},{15,13},{18,16},{19,... | collective-permute-start | bytes 3464 | tf_op jit(solution)/shard_map/ppermute | solution.py:15
  189.6 2.1 collective-permute-start.21
  191.7 1.3 collective-permute-start.20
  193.5 2.7 %collective-permute-start.23 = (f32[3,3,1,1024]{3,2,1,0:T(1,128)S(1)}, f32[3,3,1,1024]{3,2,1,0:T(1,128)S(1)}, u32[]{:S(2)}, u32[]{:S(2)}) collective-permute-start(f32[3,3,1,1024]{3,2,1,0:T(1,128)S(1)} %get-tuple-element.11), channel_id=1, source_target_pairs={{4,0},{8,4},{12,8},{16,12},{20,16},{24,20},{28,24},{5,1},{9,5},{13... | collective-permute-start | bytes 110600 | tf_op jit(solution)/shard_map/ppermute | solution.py:15
  196.2 2.6 %collective-permute-start.22 = (f32[3,3,1,1024]{3,2,1,0:T(1,128)S(1)}, f32[3,3,1,1024]{3,2,1,0:T(1,128)S(1)}, u32[]{:S(2)}, u32[]{:S(2)}) collective-permute-start(f32[3,3,1,1024]{3,2,1,0:T(1,128)S(1)} %get-tuple-element.12), channel_id=1, source_target_pairs={{0,4},{4,8},{8,12},{12,16},{16,20},{20,24},{24,28},{1,5},{5,9},{9,... | collective-permute-start | bytes 110600 | tf_op jit(solution)/shard_map/ppermute | solution.py:14
  200.3 1.8 collective-permute-done.24
  202.1 2.5 %collective-permute-done.20 = f32[3,1,32,1024]{3,2,1,0:T(8,128)S(1)} collective-permute-done((f32[3,1,32,1024]{3,2,1,0:T(8,128)S(1)}, f32[3,1,32,1024]{3,2,1,0:T(8,128)S(1)}, u32[]{:S(2)}, u32[]{:S(2)}) %collective-permute-start.20) | collective-permute-done | bytes 393248 | tf_op jit(solution)/shard_map/ppermute | solution.py:14
  204.6 1.6 fusion.53
  (90 shorter events, 21.4 us)
Async XLA Ops:
  6.5 1.2 copy-start
  6.5 2.1 copy-start.6
  6.5 111.2 %all-gather.2.cloned.1.call-start = ((), (), s32[]{:S(2)}) async-start(), calls=%async_computation.2 | async-start | bytes 4718592 | tf_op jit(solution)/shard_map/all_gather | solution.py:46
  18.6 5.8 %copy-start.7 = (bf16[32,256]{1,0:T(8,128)(2,1)S(1)}, bf16[32,256]{1,0:T(8,128)(2,1)}, u32[]{:S(2)}) copy-start(bf16[32,256]{1,0:T(8,128)(2,1)} %param.9) | copy-start | bytes 49156
  18.6 53.7 %all-to-all-start = ((bf16[8,2,24576]{2,1,0:T(2,128)(2,1)}), bf16[8,2,24576]{2,1,0:T(2,128)(2,1)S(1)}, u32[]{:S(2)}, u32[]{:S(2)}) async-start(bf16[8,2,24576]{2,1,0:T(2,128)(2,1)} %reshape.39), calls=%async_computation | async-start | bytes 1572864 | tf_op jit(solution)/shard_map/all_to_all | solution.py:52
  83.5 7.1 %copy-start.4 = (bf16[3,2,3,32,2048]{4,3,2,1,0:T(8,128)(2,1)S(1)}, bf16[3,2,3,32,2048]{4,3,2,1,0:T(8,128)(2,1)}, u32[]{:S(2)}) copy-start(bf16[3,2,3,32,2048]{4,3,2,1,0:T(8,128)(2,1)} %param.7) | copy-start | bytes 7077892
  86.0 26.2 %all-to-all-start.1 = ((bf16[8,6,32,256]{3,2,1,0:T(8,128)(2,1)}), bf16[8,6,32,256]{3,2,1,0:T(8,128)(2,1)S(1)}, u32[]{:S(2)}, u32[]{:S(2)}) async-start(bf16[8,6,32,256]{3,2,1,0:T(8,128)(2,1)} %fusion.91), calls=%async_computation.1 | async-start | bytes 1572864 | tf_op jit(solution)/shard_map/all_to_all | solution.py:58
  91.8 31.8 %collective-permute-start = (bf16[3,2,3,32,1024]{4,3,2,0,1:T(8,128)(2,1)}, bf16[3,2,3,32,1024]{4,3,2,0,1:T(8,128)(2,1)}, u32[]{:S(2)}, u32[]{:S(2)}) collective-permute-start(bf16[3,2,3,32,1024]{4,3,2,0,1:T(8,128)(2,1)} %copy.33), channel_id=1, source_target_pairs={{0,2},{2,0},{1,3},{3,1},{4,6},{6,4},{5,7},{7,5},{8,10},{10,8},{9,1... | collective-permute-start | bytes 3538952 | tf_op jit(solution)/shard_map/ppermute | solution.py:67
  113.2 8.0 %collective-permute-start.1 = (bf16[6,32,2048]{2,1,0:T(8,128)(2,1)}, bf16[6,32,2048]{2,1,0:T(8,128)(2,1)}, u32[]{:S(2)}, u32[]{:S(2)}) collective-permute-start(bf16[6,32,2048]{2,1,0:T(8,128)(2,1)} %bitcast.41), channel_id=1, source_target_pairs={{0,2},{2,0},{1,3},{3,1},{4,6},{6,4},{5,7},{7,5},{8,10},{10,8},{9,1... | collective-permute-start | bytes 2359304 | tf_op jit(solution)/shard_map/ppermute | solution.py:68
  117.7 3.5 %copy-start.2 = (bf16[2048,1024]{1,0:T(8,128)(2,1)S(1)}, bf16[2048,1024]{1,0:T(8,128)(2,1)}, u32[]{:S(2)}) copy-start(bf16[2048,1024]{1,0:T(8,128)(2,1)} %all-gather.2.cloned.1.call-done) | copy-start | bytes 12582916
  121.2 2.4 %copy-start.5 = (bf16[3,2,3,32,2048]{4,3,2,1,0:T(8,128)(2,1)S(1)}, bf16[3,2,3,32,2048]{4,3,2,1,0:T(8,128)(2,1)}, u32[]{:S(2)}) copy-start(bf16[3,2,3,32,2048]{4,3,2,1,0:T(8,128)(2,1)} %param.7) | copy-start | bytes 7077892
  126.3 11.6 %collective-permute-start.7 = (f32[3,3,32,1]{3,2,1,0:T(8,128)S(1)}, f32[3,3,32,1]{3,2,1,0:T(8,128)S(1)}, u32[]{:S(2)}, u32[]{:S(2)}) collective-permute-start(f32[3,3,32,1]{3,2,1,0:T(8,128)S(1)} %get-tuple-element.49), channel_id=1, source_target_pairs={{2,0},{3,1},{6,4},{7,5},{10,8},{11,9},{14,12},{15,13},{18,16},{19,... | collective-permute-start | bytes 3464 | tf_op jit(solution)/shard_map/ppermute | solution.py:15
  128.2 13.4 %collective-permute-start.3 = (f32[3,1,32,1024]{3,2,1,0:T(8,128)S(1)}, f32[3,1,32,1024]{3,2,1,0:T(8,128)S(1)}, u32[]{:S(2)}, u32[]{:S(2)}) collective-permute-start(f32[3,1,32,1024]{3,2,1,0:T(8,128)S(1)} %get-tuple-element.57), channel_id=1, source_target_pairs={{1,0},{3,2},{5,4},{7,6},{9,8},{11,10},{13,12},{15,14},{17,16},{19,... | collective-permute-start | bytes 1179656 | tf_op jit(solution)/shard_map/ppermute | solution.py:15
  130.4 12.9 %collective-permute-start.2 = (f32[3,1,32,1024]{3,2,1,0:T(8,128)S(1)}, f32[3,1,32,1024]{3,2,1,0:T(8,128)S(1)}, u32[]{:S(2)}, u32[]{:S(2)}) collective-permute-start(f32[3,1,32,1024]{3,2,1,0:T(8,128)S(1)} %get-tuple-element.58), channel_id=1, source_target_pairs={{0,1},{2,3},{4,5},{6,7},{8,9},{10,11},{12,13},{14,15},{16,17},{18,... | collective-permute-start | bytes 1179656 | tf_op jit(solution)/shard_map/ppermute | solution.py:14
  131.8 9.4 %collective-permute-start.5 = (f32[3,3,1,1024]{3,2,1,0:T(1,128)S(1)}, f32[3,3,1,1024]{3,2,1,0:T(1,128)S(1)}, u32[]{:S(2)}, u32[]{:S(2)}) collective-permute-start(f32[3,3,1,1024]{3,2,1,0:T(1,128)S(1)} %get-tuple-element.53), channel_id=1, source_target_pairs={{4,0},{8,4},{12,8},{16,12},{20,16},{24,20},{28,24},{5,1},{9,5},{13... | collective-permute-start | bytes 110600 | tf_op jit(solution)/shard_map/ppermute | solution.py:15
  136.0 5.6 %collective-permute-start.4 = (f32[3,3,1,1024]{3,2,1,0:T(1,128)S(1)}, f32[3,3,1,1024]{3,2,1,0:T(1,128)S(1)}, u32[]{:S(2)}, u32[]{:S(2)}) collective-permute-start(f32[3,3,1,1024]{3,2,1,0:T(1,128)S(1)} %get-tuple-element.54), channel_id=1, source_target_pairs={{0,4},{4,8},{8,12},{12,16},{16,20},{20,24},{24,28},{1,5},{5,9},{9,... | collective-permute-start | bytes 110600 | tf_op jit(solution)/shard_map/ppermute | solution.py:14
  137.9 3.3 %collective-permute-start.6 = (f32[3,3,32,1]{3,2,1,0:T(8,128)S(1)}, f32[3,3,32,1]{3,2,1,0:T(8,128)S(1)}, u32[]{:S(2)}, u32[]{:S(2)}) collective-permute-start(f32[3,3,32,1]{3,2,1,0:T(8,128)S(1)} %get-tuple-element.50), channel_id=1, source_target_pairs={{0,2},{1,3},{4,6},{5,7},{8,10},{9,11},{12,14},{13,15},{16,18},{17,... | collective-permute-start | bytes 3464 | tf_op jit(solution)/shard_map/ppermute | solution.py:14
  145.0 1.1 copy-start.3
  146.7 12.7 %collective-permute-start.13 = (f32[3,3,32,1]{3,2,1,0:T(8,128)S(1)}, f32[3,3,32,1]{3,2,1,0:T(8,128)S(1)}, u32[]{:S(2)}, u32[]{:S(2)}) collective-permute-start(f32[3,3,32,1]{3,2,1,0:T(8,128)S(1)} %get-tuple-element.31), channel_id=1, source_target_pairs={{2,0},{3,1},{6,4},{7,5},{10,8},{11,9},{14,12},{15,13},{18,16},{19,... | collective-permute-start | bytes 3464 | tf_op jit(solution)/shard_map/ppermute | solution.py:15
  149.1 13.5 %collective-permute-start.9 = (f32[3,1,32,1024]{3,2,1,0:T(8,128)S(1)}, f32[3,1,32,1024]{3,2,1,0:T(8,128)S(1)}, u32[]{:S(2)}, u32[]{:S(2)}) collective-permute-start(f32[3,1,32,1024]{3,2,1,0:T(8,128)S(1)} %get-tuple-element.39), channel_id=1, source_target_pairs={{1,0},{3,2},{5,4},{7,6},{9,8},{11,10},{13,12},{15,14},{17,16},{19,... | collective-permute-start | bytes 1179656 | tf_op jit(solution)/shard_map/ppermute | solution.py:15
  152.3 12.9 %collective-permute-start.8 = (f32[3,1,32,1024]{3,2,1,0:T(8,128)S(1)}, f32[3,1,32,1024]{3,2,1,0:T(8,128)S(1)}, u32[]{:S(2)}, u32[]{:S(2)}) collective-permute-start(f32[3,1,32,1024]{3,2,1,0:T(8,128)S(1)} %get-tuple-element.40), channel_id=1, source_target_pairs={{0,1},{2,3},{4,5},{6,7},{8,9},{10,11},{12,13},{14,15},{16,17},{18,... | collective-permute-start | bytes 1179656 | tf_op jit(solution)/shard_map/ppermute | solution.py:14
  154.1 8.6 %collective-permute-start.11 = (f32[3,3,1,1024]{3,2,1,0:T(1,128)S(1)}, f32[3,3,1,1024]{3,2,1,0:T(1,128)S(1)}, u32[]{:S(2)}, u32[]{:S(2)}) collective-permute-start(f32[3,3,1,1024]{3,2,1,0:T(1,128)S(1)} %get-tuple-element.35), channel_id=1, source_target_pairs={{4,0},{8,4},{12,8},{16,12},{20,16},{24,20},{28,24},{5,1},{9,5},{13... | collective-permute-start | bytes 110600 | tf_op jit(solution)/shard_map/ppermute | solution.py:15
  156.8 5.9 %collective-permute-start.10 = (f32[3,3,1,1024]{3,2,1,0:T(1,128)S(1)}, f32[3,3,1,1024]{3,2,1,0:T(1,128)S(1)}, u32[]{:S(2)}, u32[]{:S(2)}) collective-permute-start(f32[3,3,1,1024]{3,2,1,0:T(1,128)S(1)} %get-tuple-element.36), channel_id=1, source_target_pairs={{0,4},{4,8},{8,12},{12,16},{16,20},{20,24},{24,28},{1,5},{5,9},{9,... | collective-permute-start | bytes 110600 | tf_op jit(solution)/shard_map/ppermute | solution.py:14
  159.4 3.3 %collective-permute-start.12 = (f32[3,3,32,1]{3,2,1,0:T(8,128)S(1)}, f32[3,3,32,1]{3,2,1,0:T(8,128)S(1)}, u32[]{:S(2)}, u32[]{:S(2)}) collective-permute-start(f32[3,3,32,1]{3,2,1,0:T(8,128)S(1)} %get-tuple-element.32), channel_id=1, source_target_pairs={{0,2},{1,3},{4,6},{5,7},{8,10},{9,11},{12,14},{13,15},{16,18},{17,... | collective-permute-start | bytes 3464 | tf_op jit(solution)/shard_map/ppermute | solution.py:14
  167.5 11.6 %collective-permute-start.19 = (f32[3,3,32,1]{3,2,1,0:T(8,128)S(1)}, f32[3,3,32,1]{3,2,1,0:T(8,128)S(1)}, u32[]{:S(2)}, u32[]{:S(2)}) collective-permute-start(f32[3,3,32,1]{3,2,1,0:T(8,128)S(1)} %get-tuple-element.19), channel_id=1, source_target_pairs={{2,0},{3,1},{6,4},{7,5},{10,8},{11,9},{14,12},{15,13},{18,16},{19,... | collective-permute-start | bytes 3464 | tf_op jit(solution)/shard_map/ppermute | solution.py:15
  169.9 12.5 %collective-permute-start.15 = (f32[3,1,32,1024]{3,2,1,0:T(8,128)S(1)}, f32[3,1,32,1024]{3,2,1,0:T(8,128)S(1)}, u32[]{:S(2)}, u32[]{:S(2)}) collective-permute-start(f32[3,1,32,1024]{3,2,1,0:T(8,128)S(1)} %get-tuple-element.27), channel_id=1, source_target_pairs={{1,0},{3,2},{5,4},{7,6},{9,8},{11,10},{13,12},{15,14},{17,16},{19,... | collective-permute-start | bytes 1179656 | tf_op jit(solution)/shard_map/ppermute | solution.py:15
  172.0 12.9 %collective-permute-start.14 = (f32[3,1,32,1024]{3,2,1,0:T(8,128)S(1)}, f32[3,1,32,1024]{3,2,1,0:T(8,128)S(1)}, u32[]{:S(2)}, u32[]{:S(2)}) collective-permute-start(f32[3,1,32,1024]{3,2,1,0:T(8,128)S(1)} %get-tuple-element.28), channel_id=1, source_target_pairs={{0,1},{2,3},{4,5},{6,7},{8,9},{10,11},{12,13},{14,15},{16,17},{18,... | collective-permute-start | bytes 1179656 | tf_op jit(solution)/shard_map/ppermute | solution.py:14
  173.8 8.6 %collective-permute-start.17 = (f32[3,3,1,1024]{3,2,1,0:T(1,128)S(1)}, f32[3,3,1,1024]{3,2,1,0:T(1,128)S(1)}, u32[]{:S(2)}, u32[]{:S(2)}) collective-permute-start(f32[3,3,1,1024]{3,2,1,0:T(1,128)S(1)} %get-tuple-element.23), channel_id=1, source_target_pairs={{4,0},{8,4},{12,8},{16,12},{20,16},{24,20},{28,24},{5,1},{9,5},{13... | collective-permute-start | bytes 110600 | tf_op jit(solution)/shard_map/ppermute | solution.py:15
  176.5 5.9 %collective-permute-start.16 = (f32[3,3,1,1024]{3,2,1,0:T(1,128)S(1)}, f32[3,3,1,1024]{3,2,1,0:T(1,128)S(1)}, u32[]{:S(2)}, u32[]{:S(2)}) collective-permute-start(f32[3,3,1,1024]{3,2,1,0:T(1,128)S(1)} %get-tuple-element.24), channel_id=1, source_target_pairs={{0,4},{4,8},{8,12},{12,16},{16,20},{20,24},{24,28},{1,5},{5,9},{9,... | collective-permute-start | bytes 110600 | tf_op jit(solution)/shard_map/ppermute | solution.py:14
  179.1 3.3 %collective-permute-start.18 = (f32[3,3,32,1]{3,2,1,0:T(8,128)S(1)}, f32[3,3,32,1]{3,2,1,0:T(8,128)S(1)}, u32[]{:S(2)}, u32[]{:S(2)}) collective-permute-start(f32[3,3,32,1]{3,2,1,0:T(8,128)S(1)} %get-tuple-element.20), channel_id=1, source_target_pairs={{0,2},{1,3},{4,6},{5,7},{8,10},{9,11},{12,14},{13,15},{16,18},{17,... | collective-permute-start | bytes 3464 | tf_op jit(solution)/shard_map/ppermute | solution.py:14
  187.2 11.6 %collective-permute-start.25 = (f32[3,3,32,1]{3,2,1,0:T(8,128)S(1)}, f32[3,3,32,1]{3,2,1,0:T(8,128)S(1)}, u32[]{:S(2)}, u32[]{:S(2)}) collective-permute-start(f32[3,3,32,1]{3,2,1,0:T(8,128)S(1)} %get-tuple-element.7), channel_id=1, source_target_pairs={{2,0},{3,1},{6,4},{7,5},{10,8},{11,9},{14,12},{15,13},{18,16},{19,... | collective-permute-start | bytes 3464 | tf_op jit(solution)/shard_map/ppermute | solution.py:15
  189.6 12.5 %collective-permute-start.21 = (f32[3,1,32,1024]{3,2,1,0:T(8,128)S(1)}, f32[3,1,32,1024]{3,2,1,0:T(8,128)S(1)}, u32[]{:S(2)}, u32[]{:S(2)}) collective-permute-start(f32[3,1,32,1024]{3,2,1,0:T(8,128)S(1)} %get-tuple-element.15), channel_id=1, source_target_pairs={{1,0},{3,2},{5,4},{7,6},{9,8},{11,10},{13,12},{15,14},{17,16},{19,... | collective-permute-start | bytes 1179656 | tf_op jit(solution)/shard_map/ppermute | solution.py:15
  191.7 12.9 %collective-permute-start.20 = (f32[3,1,32,1024]{3,2,1,0:T(8,128)S(1)}, f32[3,1,32,1024]{3,2,1,0:T(8,128)S(1)}, u32[]{:S(2)}, u32[]{:S(2)}) collective-permute-start(f32[3,1,32,1024]{3,2,1,0:T(8,128)S(1)} %get-tuple-element.16), channel_id=1, source_target_pairs={{0,1},{2,3},{4,5},{6,7},{8,9},{10,11},{12,13},{14,15},{16,17},{18,... | collective-permute-start | bytes 1179656 | tf_op jit(solution)/shard_map/ppermute | solution.py:14
  193.5 8.6 %collective-permute-start.23 = (f32[3,3,1,1024]{3,2,1,0:T(1,128)S(1)}, f32[3,3,1,1024]{3,2,1,0:T(1,128)S(1)}, u32[]{:S(2)}, u32[]{:S(2)}) collective-permute-start(f32[3,3,1,1024]{3,2,1,0:T(1,128)S(1)} %get-tuple-element.11), channel_id=1, source_target_pairs={{4,0},{8,4},{12,8},{16,12},{20,16},{24,20},{28,24},{5,1},{9,5},{13... | collective-permute-start | bytes 110600 | tf_op jit(solution)/shard_map/ppermute | solution.py:15
  196.2 5.9 %collective-permute-start.22 = (f32[3,3,1,1024]{3,2,1,0:T(1,128)S(1)}, f32[3,3,1,1024]{3,2,1,0:T(1,128)S(1)}, u32[]{:S(2)}, u32[]{:S(2)}) collective-permute-start(f32[3,3,1,1024]{3,2,1,0:T(1,128)S(1)} %get-tuple-element.12), channel_id=1, source_target_pairs={{0,4},{4,8},{8,12},{12,16},{16,20},{20,24},{24,28},{1,5},{5,9},{9,... | collective-permute-start | bytes 110600 | tf_op jit(solution)/shard_map/ppermute | solution.py:14
  198.8 3.3 %collective-permute-start.24 = (f32[3,3,32,1]{3,2,1,0:T(8,128)S(1)}, f32[3,3,32,1]{3,2,1,0:T(8,128)S(1)}, u32[]{:S(2)}, u32[]{:S(2)}) collective-permute-start(f32[3,3,32,1]{3,2,1,0:T(8,128)S(1)} %get-tuple-element.8), channel_id=1, source_target_pairs={{0,2},{1,3},{4,6},{5,7},{8,10},{9,11},{12,14},{13,15},{16,18},{17,... | collective-permute-start | bytes 3464 | tf_op jit(solution)/shard_map/ppermute | solution.py:14
  206.3 1.4 copy-start.1
Sparse Core Ops, SparseCore 0:
  9.5 89.8 all-gather.1
